TPU v7x, 32 devices: a whole 2x2x4 slice. The times are simulated.
32 devices in a mesh: grp: 2 (over y), row: 4 (over z), col: 4 (over x, core).
Axes of the slice: x: 2, y: 2, z: 4, core: 2. Of those that a mesh axis runs over, the one named last changes fastest.
Arguments:
- hessian_old: float32 [18432, 9216], P(('grp', 'row'), 'col'), parts along dimension 0, may hold values from -8 to 48, as said below
- tokens: bfloat16 [128, 9216], P(('grp', 'row'), 'col'), parts along dimension 0, may hold values from -6 to 6
- weight: float32 [128, 9216], P(('grp', 'row'), 'col'), parts along dimension 0, may hold values from -6 to 6
- dense_weight: float32 [128, 9216], P(('grp', 'row'), 'col'), parts along dimension 0, may hold values from -6 to 6
- block_mask: int32 [128, 72], P(('grp', 'row'), 'col'), parts along dimension 0, may hold values 0 or 1
Outputs:
- hessian: float32 [18432, 9216], P(('grp', 'row'), 'col'), parts along dimension 0
- new_weight: float32 [128, 9216], P(('grp', 'row'), 'col'), parts along dimension 0
There are 2 independent parts, one for each index of `grp`. A program takes and returns all parts, laid end to end along the dimension named above; each array names one. Nothing has to cross between parts.
Inputs may be any that keep to these rules, and one draw needn't show every extreme that they name: hessian_old is symmetric and has a positive diagonal.
All inputs are finite; a program needn't handle non-finite values. No bound on the sum of `block_mask` on one device may be relied on, other than what follows from the above.
Results may differ from a plain program's by a relative error of at most 0.0035.
Values may be sent and summed in bfloat16 or wider, within the bound.
A program may use at most 128 MiB of HBM per device.

v0:
```python
import functools

import jax
import jax.numpy as jnp
from jax import lax
from jax.experimental import pallas as pl
from jax.experimental.pallas import tpu as pltpu
from jax.sharding import PartitionSpec as P

MESH = pl.DeviceIdType.MESH


def general(hessian_old, tokens, weight, dense_weight, block_mask):
    row_tile = hessian_old.shape[0]
    col_tile = hessian_old.shape[1]
    row_idx = lax.axis_index("row")
    col_idx = lax.axis_index("col")
    col_panel = lax.all_gather(tokens, "row", axis=0, tiled=True)
    features = lax.all_gather(tokens, "col", axis=1, tiled=True)
    row_panel = lax.all_to_all(features, "row", split_axis=1, concat_axis=0, tiled=True)
    gram_tile = lax.dot_general(
        row_panel, col_panel, (((0,), (0,)), ((), ())), preferred_element_type=jnp.float32
    )
    token_count = tokens.shape[0] * lax.axis_size("row")
    hessian = hessian_old + gram_tile / token_count
    row_ids = lax.broadcasted_iota(jnp.int32, (row_tile, col_tile), 0) + row_idx * row_tile
    col_ids = lax.broadcasted_iota(jnp.int32, (row_tile, col_tile), 1) + col_idx * col_tile
    local_trace = jnp.sum(jnp.where(row_ids == col_ids, hessian, jnp.float32(0.0)))
    diag_sum = lax.psum(local_trace, ("row", "col"))
    weight_rows = weight.shape[0]
    block_count = block_mask.shape[1]
    block_width = col_tile // block_count
    kept_mask = (
        block_mask.astype(jnp.float32)[:, :, None] * jnp.ones((1, 1, block_width), jnp.float32)
    ).reshape(weight_rows, col_tile)
    difference = (kept_mask * weight - dense_weight).astype(jnp.bfloat16)
    hess_low = hessian.astype(jnp.bfloat16)
    partial_grad = lax.dot_general(
        lax.all_gather(difference, "row", axis=0, tiled=True),
        hess_low,
        (((1,), (1,)), ((), ())),
        preferred_element_type=jnp.float32,
    )
    spread = lax.all_to_all(partial_grad, "row", split_axis=0, concat_axis=1, tiled=True)
    gradient = lax.psum_scatter(spread, "col", scatter_dimension=1, tiled=True)
    step_size = 0.25 * (row_tile * lax.axis_size("row")) / diag_sum
    new_weight = kept_mask * (weight - step_size * gradient)
    return (hessian, new_weight)


def hail(devices):
    barrier = pltpu.get_barrier_semaphore()
    for device in devices:
        pl.semaphore_signal(barrier, inc=1, device_id=device, device_id_type=MESH)


def meet(count):
    pl.semaphore_wait(pltpu.get_barrier_semaphore(), count)


def remote(src, dst, send_sem, recv_sem, device):
    return pltpu.make_async_remote_copy(
        src_ref=src, dst_ref=dst, send_sem=send_sem, recv_sem=recv_sem,
        device_id=device, device_id_type=MESH,
    )


def gather_kernel(
    n, old_hbm, tok_hbm, w_hbm, d_hbm, m_hbm, old, colp, rowt, rowd, tok_ref, w_ref, d_ref, m_ref, diff,
    in_sem, send_a, send_d, send_b, send_r, recv_a, recv_d, recv_b,
):
    g, r, c = lax.axis_index("grp"), lax.axis_index("row"), lax.axis_index("col")
    loads = [
        pltpu.make_async_copy(src, dst, in_sem.at[i])
        for i, (src, dst) in enumerate(
            [(w_hbm, w_ref), (d_hbm, d_ref), (m_hbm, m_ref), (tok_hbm, tok_ref), (old_hbm, old)]
        )
    ]
    for load in loads:
        load.start()
    others = [lax.rem(r + j, n) for j in range(1, n)]
    beside = [lax.rem(c + j, n) for j in range(1, n)]
    hail([(g, rr, c) for rr in others] + [(g, r, cc) for cc in beside])
    for load in loads[:4]:
        load.wait()
    blocks = m_ref.shape[1]
    width = tok_ref.shape[1] // blocks
    for b in range(blocks):
        at = slice(b * width, (b + 1) * width)
        kept = m_ref[:, b : b + 1].astype(jnp.float32)
        diff[:, at] = (kept * w_ref[:, at] - d_ref[:, at]).astype(jnp.bfloat16)
    meet(len(others) + len(beside))

    root = r == c
    partner = c + 1 - 2 * lax.rem(c, 2)
    partner_dev = (g, r, partner)
    twins = [(g, r, lax.rem(c + 2 * j, n)) for j in range(1, n // 2)]
    even = lax.rem(r, 2) == lax.rem(c, 2)

    mate = partner
    crosses = r // 2 != c // 2

    def direct(rr):
        return jnp.logical_and(rr != r, jnp.logical_not(jnp.logical_and(crosses, rr == mate)))

    def relay(s):
        return s // 2 != r // 2, remote(
            colp.at[s], colp.at[s], send_r.at[s], recv_a.at[s], (g, mate, c)
        )

    def token_copy(k):
        rr = lax.rem(c + k, n)
        return rr, remote(tok_ref, colp.at[r], send_a.at[k], recv_a.at[r], (g, rr, c))

    diff_copy = remote(diff, rowd.at[r], send_d, recv_d.at[r], (g, c, c))

    @pl.when(jnp.logical_not(root))
    def _():
        token_copy(0)[1].start()
        diff_copy.start()

    def spread(s, token_src, diff_src, devices, start):
        for i, device in enumerate(devices):
            one = remote(token_src, rowt.at[s], send_b.at[i, 0, s], recv_b.at[0, s], device)
            two = remote(diff_src, rowd.at[s], send_b.at[i, 1, s], recv_b.at[1, s], device)
            if start:
                one.start()
                two.start()
            else:
                one.wait_send()
                two.wait_send()

    @pl.when(root)
    def _():
        spread(r, tok_ref, diff, twins + [partner_dev], True)

    for k in range(1, n):
        rr, copy = token_copy(k)

        @pl.when(direct(rr))
        def _():
            copy.start()

    colp[r] = tok_ref[...]

    def got_a(s):
        remote(tok_ref, colp.at[s], send_a.at[0], recv_a.at[s], partner_dev).wait_recv()

    def got_d(s):
        remote(diff, rowd.at[s], send_d, recv_d.at[s], partner_dev).wait_recv()

    def got_b(s):
        remote(tok_ref, rowt.at[s], send_d, recv_b.at[0, s], partner_dev).wait_recv()
        remote(diff, rowd.at[s], send_d, recv_b.at[1, s], partner_dev).wait_recv()

    @pl.when(root)
    def _():
        for s in others:
            got_a(s)
            got_d(s)
            spread(s, colp.at[s], rowd.at[s], twins + [partner_dev], True)
            far, copy = relay(s)

            @pl.when(far)
            def _():
                copy.start()

        rowd[r] = diff[...]
        for s in range(n):
            rowt[s] = colp[s]
        spread(r, tok_ref, diff, twins + [partner_dev], False)
        for s in others:
            spread(s, colp.at[s], rowd.at[s], twins + [partner_dev], False)
            far, copy = relay(s)

            @pl.when(far)
            def _():
                copy.wait_send()


    @pl.when(jnp.logical_not(root))
    def _():
        @pl.when(even)
        def _():
            for s in [r] + others:
                got_b(s)
                spread(s, rowt.at[s], rowd.at[s], [partner_dev], True)
            for s in [r] + others:
                spread(s, rowt.at[s], rowd.at[s], [partner_dev], False)

        @pl.when(jnp.logical_not(even))
        def _():
            for s in [r] + others:
                got_b(s)

        for s in others:
            got_a(s)
        diff_copy.wait_send()

    for k in range(n):
        rr, copy = token_copy(k)

        @pl.when(direct(rr))
        def _():
            copy.wait_send()

    loads[4].wait()


def scaled(value, count):
    exact = count & (count - 1) == 0
    return value * (1.0 / count) if exact else value / count


def main_kernel(
    n, rows, token_count, old_ref, rt_ref, rd_ref, cp_ref, out_hbm, part_ref, trace_ref, acc, out, out_sem
):
    tile = old_ref.shape[0]
    steps = tile // rows
    slots = out.shape[0]
    acc[...] = jnp.zeros_like(acc)
    trace_ref[...] = jnp.zeros_like(trace_ref)
    same = lax.broadcasted_iota(jnp.int32, (rows, rows), 0) == lax.broadcasted_iota(
        jnp.int32, (rows, rows), 1
    )

    def store(i):
        return pltpu.make_async_copy(
            out.at[lax.rem(i, slots)],
            out_hbm.at[pl.ds(pl.multiple_of(i * rows, rows), rows), :],
            out_sem.at[lax.rem(i, slots)],
        )

    @pl.loop(0, steps)
    def _(i):
        slot = lax.rem(i, slots)

        @pl.when(i >= slots)
        def _():
            store(i - slots).wait()

        here = pl.ds(pl.multiple_of(i * rows, rows), rows)
        gram = lax.dot_general(
            rt_ref[:, here], cp_ref[...], (((0,), (0,)), ((), ())), preferred_element_type=jnp.float32
        )
        hess = old_ref[here, :] + scaled(gram, token_count)
        out[slot] = hess
        acc[...] += jnp.dot(
            rd_ref[:, here], hess.astype(jnp.bfloat16), preferred_element_type=jnp.float32
        )
        store(i).start()

        @pl.when(lax.axis_index("row") == lax.axis_index("col"))
        def _():
            diag = jnp.where(same, out[slot, :, here], 0.0)
            total = jnp.sum(diag.reshape(rows // 8, 8, rows), axis=0)
            for b in range(rows // 128):
                trace_ref[...] += total[:, b * 128 : (b + 1) * 128]

    part_ref[...] = acc[...].astype(part_ref.dtype)
    for k in range(min(slots, steps)):
        store(jnp.int32(steps - 1 - k)).wait()


def step_kernel(n, size, part_ref, w_ref, m_ref, trace_ref, out_ref, got, traces, send_p, send_t, recv_p, recv_t):
    g, r, c = lax.axis_index("grp"), lax.axis_index("row"), lax.axis_index("col")
    others = [lax.rem(r + j, n) for j in range(1, n)]
    far = [
        (g, lax.rem(r + j, n), lax.rem(c + k, n)) for j in range(n) for k in range(n) if j or k
    ]
    hail(far)
    meet(len(far))
    sends = [
        remote(part_ref.at[s], got.at[r], send_p.at[j], recv_p.at[r], (g, s, c))
        for j, s in enumerate(others)
    ]
    tells = [
        remote(trace_ref, traces.at[r], send_t.at[j], recv_t.at[r], device)
        for j, device in enumerate(far)
    ]

    @pl.when(r == c)
    def _():
        for copy in tells:
            copy.start()

    for copy in sends:
        copy.start()

    total = jnp.zeros(trace_ref.shape, jnp.float32)
    for s in range(n):
        @pl.when(jnp.logical_or(r != c, s != r))
        def _():
            remote(trace_ref, traces.at[s], send_t.at[0], recv_t.at[s], far[0]).wait_recv()

    @pl.when(r == c)
    def _():
        traces[r] = trace_ref[...]

    for s in range(n):
        total = total + traces[s]
    step = 0.25 * size / jnp.sum(total, axis=(0, 1), keepdims=True)
    for s in others:
        remote(part_ref.at[0], got.at[s], send_p.at[0], recv_p.at[s], far[0]).wait_recv()
    got[r] = part_ref[r]
    blocks = m_ref.shape[1]
    width = w_ref.shape[1] // blocks
    for b in range(blocks):
        at = slice(b * width, (b + 1) * width)
        grad = got[0, :, at].astype(jnp.float32)
        for s in range(1, n):
            grad = grad + got[s, :, at].astype(jnp.float32)
        kept = m_ref[:, b : b + 1].astype(jnp.float32)
        out_ref[:, at] = kept * (w_ref[:, at] - step * grad)
    for copy in sends:
        copy.wait_send()

    @pl.when(r == c)
    def _():
        for copy in tells:
            copy.wait_send()


def fused(n, hessian_old, tokens, weight, dense_weight, block_mask):
    tile = hessian_old.shape[0]
    held = tokens.shape[0]
    depth = weight.shape[0]
    vmem = pl.BlockSpec(memory_space=pltpu.VMEM)
    dma = pltpu.SemaphoreType.DMA
    hbm = pl.BlockSpec(memory_space=pltpu.HBM)
    old, colp, rowt, rowd = pl.pallas_call(
        functools.partial(gather_kernel, n),
        out_shape=(
            jax.ShapeDtypeStruct((tile, tile), jnp.float32),
            jax.ShapeDtypeStruct((n, held, tile), jnp.bfloat16),
            jax.ShapeDtypeStruct((n, held, tile), jnp.bfloat16),
            jax.ShapeDtypeStruct((n, depth, tile), jnp.bfloat16),
        ),
        in_specs=[hbm] * 5,
        out_specs=(vmem,) * 4,
        scratch_shapes=[
            pltpu.VMEM((held, tile), jnp.bfloat16),
            pltpu.VMEM((depth, tile), jnp.float32),
            pltpu.VMEM((depth, tile), jnp.float32),
            pltpu.VMEM(block_mask.shape, jnp.int32),
            pltpu.VMEM((depth, tile), jnp.bfloat16),
            dma((5,)),
            dma((n,)),
            dma,
            dma((n // 2, 2, n)),
            dma((n,)),
            dma((n,)),
            dma((n,)),
            dma((2, n)),
        ],
        compiler_params=pltpu.CompilerParams(
            collective_id=0, has_side_effects=True, vmem_limit_bytes=4 << 20
        ),
    )(*[pltpu.with_memory_space_constraint(x, pltpu.HBM) for x in (hessian_old, tokens, weight, dense_weight, block_mask)])
    colp = colp.reshape(n * held, tile)
    rowt = rowt.reshape(n * held, tile)
    rowd = rowd.reshape(n * depth, tile)
    rows = 256 if tile % 256 == 0 else 128
    hessian, partial, trace = pl.pallas_call(
        functools.partial(main_kernel, n, rows, n * held),
        out_shape=(
            jax.ShapeDtypeStruct((tile, tile), jnp.float32),
            jax.ShapeDtypeStruct((n * depth, tile), jnp.bfloat16),
            jax.ShapeDtypeStruct((8, 128), jnp.float32),
        ),
        in_specs=[vmem] * 4,
        out_specs=(hbm, vmem, vmem),
        scratch_shapes=[
            pltpu.VMEM((n * depth, tile), jnp.float32),
            pltpu.VMEM((3, rows, tile), jnp.float32),
            dma((3,)),
        ],
        compiler_params=pltpu.CompilerParams(vmem_limit_bytes=16 << 20),
    )(old, rowt, rowd, colp)
    new_weight = pl.pallas_call(
        functools.partial(step_kernel, n, tile * n),
        out_shape=jax.ShapeDtypeStruct((depth, tile), jnp.float32),
        in_specs=[vmem] * 4,
        out_specs=vmem,
        scratch_shapes=[
            pltpu.VMEM((n, depth, tile), jnp.bfloat16),
            pltpu.VMEM((n, 8, 128), jnp.float32),
            dma((n - 1,)),
            dma((n * n - 1,)),
            dma((n,)),
            dma((n,)),
        ],
        compiler_params=pltpu.CompilerParams(
            collective_id=1, has_side_effects=True, vmem_limit_bytes=8 << 20
        ),
    )(partial.reshape(n, depth, tile), weight, block_mask, trace)
    return hessian, new_weight


def solution(mesh):
    n = mesh.shape["row"]

    def on_device(hessian_old, tokens, weight, dense_weight, block_mask):
        tile = hessian_old.shape[0]
        fits = (
            n == mesh.shape["col"]
            and n > 1
            and n % 2 == 0
            and tile == hessian_old.shape[1]
            and tile % 128 == 0
            and tile == block_mask.shape[1] * 128
            and tokens.shape[0] % 16 == 0
            and weight.shape[0] % 16 == 0
        )
        args = (hessian_old, tokens, weight, dense_weight, block_mask)
        return fused(n, *args) if fits else general(*args)

    spec = P(("grp", "row"), "col")
    return jax.shard_map(
        on_device, mesh=mesh, in_specs=(spec,) * 5, out_specs=(spec, spec), check_vma=False
    )
```

profile of v0, /device:TPU:0, one launch (start us, length us, event | category | flops | bytes accessed | tf_op | source)
XLA Modules:
  0.0 39.5 jit_solution(12782383497921203903)
XLA Ops:
  0.6 0.0 copy-start.1
  0.6 0.0 copy-start
  0.7 17.6 %shard_map.68 = (f32[2304,2304]{1,0:T(8,128)S(1)}, bf16[4,16,2304]{2,1,0:T(8,128)(2,1)S(1)}, bf16[4,16,2304]{2,1,0:T(8,128)(2,1)S(1)}, bf16[4,16,2304]{2,1,0:T(8,128)(2,1)S(1)}) custom-call(f32[2304,2304]{1,0:T(8,128)} %old_hbm.1, bf16[16,2304]{1,0:T(8,128)(2,1)} %tok_hbm.1, f32[16,2304]{1,0:T(8,128)} %w_ref.1, f32[16,2304]{1,0:T(8,128)} %d_hbm.1, ...), custom_call_target="tpu_custom_call" | custom-call | tf_op jit(solution)/shard_map/pallas_call | solution.py:331
  18.2 7.9 %shard_map.69 = (f32[2304,2304]{1,0:T(8,128)}, bf16[64,2304]{1,0:T(8,128)(2,1)S(1)}, f32[8,128]{1,0:T(8,128)S(1)}) custom-call(f32[2304,2304]{1,0:T(8,128)S(1)} %get-tuple-element.9.old_ref, bf16[64,2304]{1,0:T(8,128)(2,1)S(1)} %bitcast.6, bf16[64,2304]{1,0:T(8,128)(2,1)S(1)} %bitcast.7, bf16[64,2304]{1,0:T(8,128)(2,1)S(1)} %bitcast.5), custom_call_target="tpu_custom_call" | custom-call | tf_op jit(solution)/shard_map/pallas_call | solution.py:364
  26.1 0.0 copy-done.1
  26.1 0.0 copy-done
  26.1 12.7 %shard_map.70 = f32[16,2304]{1,0:T(8,128)S(1)} custom-call(bf16[4,16,2304]{2,1,0:T(8,128)(2,1)S(1)} %bitcast.4, f32[16,2304]{1,0:T(8,128)S(1)} %copy-done, s32[16,18]{1,0:T(8,128)S(1)} %copy-done.1, f32[8,128]{1,0:T(8,128)S(1)} %get-tuple-element.15.trace_ref), custom_call_target="tpu_custom_call" | custom-call | tf_op jit(solution)/shard_map/pallas_call | solution.py:380
  38.8 0.7 %copy.8 = f32[16,2304]{1,0:T(8,128)} copy(f32[16,2304]{1,0:T(8,128)S(1)} %shard_map.70) | data formatting | bytes 294912
Async XLA Ops:
  0.6 25.5 %copy-start.1 = (s32[16,18]{1,0:T(8,128)S(1)}, s32[16,18]{1,0:T(8,128)}, u32[]{:S(2)}) copy-start(s32[16,18]{1,0:T(8,128)} %m_ref.1) | copy-start | bytes 3460
  0.6 25.5 %copy-start = (f32[16,2304]{1,0:T(8,128)S(1)}, f32[16,2304]{1,0:T(8,128)}, u32[]{:S(2)}) copy-start(f32[16,2304]{1,0:T(8,128)} %w_ref.1) | copy-start | bytes 442372
where the time goes:
time: 39.6 us; the launch traced here: 39.5 us
  Pallas kernels  38.1 us (96%)
  between operations  0.69 us (2%)
  local copies, waits for them, and re-layouts  0.67 us (2%)
    pallas_call x1, Pallas kernels, fused(): pl.pallas_call(functools.partial(gather_kernel, n), out_shape=(jax.ShapeD...  17.6 us
    pallas_call x1, Pallas kernels, fused(): pl.pallas_call(functools.partial(step_kernel, n, tile * n), out_shape=jax...  12.7 us
    pallas_call x1, Pallas kernels, fused(): pl.pallas_call(functools.partial(main_kernel, n, rows, n * held), out_sha...  7.87 us

commit v1 on v0

v1 whole, which is shorter than its diff:
```python
import functools

import jax
import jax.numpy as jnp
from jax import lax
from jax.experimental import pallas as pl
from jax.experimental.pallas import tpu as pltpu
from jax.sharding import PartitionSpec as P

MESH = pl.DeviceIdType.MESH


def general(hessian_old, tokens, weight, dense_weight, block_mask):
    row_tile = hessian_old.shape[0]
    col_tile = hessian_old.shape[1]
    row_idx = lax.axis_index("row")
    col_idx = lax.axis_index("col")
    col_panel = lax.all_gather(tokens, "row", axis=0, tiled=True)
    features = lax.all_gather(tokens, "col", axis=1, tiled=True)
    row_panel = lax.all_to_all(features, "row", split_axis=1, concat_axis=0, tiled=True)
    gram_tile = lax.dot_general(
        row_panel, col_panel, (((0,), (0,)), ((), ())), preferred_element_type=jnp.float32
    )
    token_count = tokens.shape[0] * lax.axis_size("row")
    hessian = hessian_old + gram_tile / token_count
    row_ids = lax.broadcasted_iota(jnp.int32, (row_tile, col_tile), 0) + row_idx * row_tile
    col_ids = lax.broadcasted_iota(jnp.int32, (row_tile, col_tile), 1) + col_idx * col_tile
    local_trace = jnp.sum(jnp.where(row_ids == col_ids, hessian, jnp.float32(0.0)))
    diag_sum = lax.psum(local_trace, ("row", "col"))
    weight_rows = weight.shape[0]
    block_count = block_mask.shape[1]
    block_width = col_tile // block_count
    kept_mask = (
        block_mask.astype(jnp.float32)[:, :, None] * jnp.ones((1, 1, block_width), jnp.float32)
    ).reshape(weight_rows, col_tile)
    difference = (kept_mask * weight - dense_weight).astype(jnp.bfloat16)
    hess_low = hessian.astype(jnp.bfloat16)
    partial_grad = lax.dot_general(
        lax.all_gather(difference, "row", axis=0, tiled=True),
        hess_low,
        (((1,), (1,)), ((), ())),
        preferred_element_type=jnp.float32,
    )
    spread = lax.all_to_all(partial_grad, "row", split_axis=0, concat_axis=1, tiled=True)
    gradient = lax.psum_scatter(spread, "col", scatter_dimension=1, tiled=True)
    step_size = 0.25 * (row_tile * lax.axis_size("row")) / diag_sum
    new_weight = kept_mask * (weight - step_size * gradient)
    return (hessian, new_weight)


def hail(devices):
    barrier = pltpu.get_barrier_semaphore()
    for device in devices:
        pl.semaphore_signal(barrier, inc=1, device_id=device, device_id_type=MESH)


def meet(count):
    pl.semaphore_wait(pltpu.get_barrier_semaphore(), count)


def remote(src, dst, send_sem, recv_sem, device):
    return pltpu.make_async_remote_copy(
        src_ref=src, dst_ref=dst, send_sem=send_sem, recv_sem=recv_sem,
        device_id=device, device_id_type=MESH,
    )


def scaled(value, count):
    exact = count & (count - 1) == 0
    return value * (1.0 / count) if exact else value / count


def exchange_kernel(
    n, parts, old_hbm, tok_hbm, w_hbm, d_hbm, m_hbm,
    old, colp, rowt, gsum, mgot, tgot,
    tok_ref, w_ref, d_ref, m_ref, diff, cold, part, pout, pgot, gred, mine, trow, tsum,
    in_sem, old_sem, send_l, recv_l, relay_l, send_x, recv_x, send_p, recv_p, send_f, recv_f,
    send_m, recv_m, send_t, recv_t, send_u, recv_u,
):
    g, r, c = lax.axis_index("grp"), lax.axis_index("row"), lax.axis_index("col")
    tile = old.shape[0]
    depth = diff.shape[0]
    held = tok_ref.shape[0]
    span = tile // parts
    loads = [
        pltpu.make_async_copy(src, dst, in_sem.at[i])
        for i, (src, dst) in enumerate([(w_hbm, w_ref), (d_hbm, d_ref), (m_hbm, m_ref), (tok_hbm, tok_ref)])
    ]
    for load in loads:
        load.start()
    stripes = [slice(p * span, (p + 1) * span) for p in range(parts)]
    olds = [
        pltpu.make_async_copy(old_hbm.at[at, :], old.at[at, :], old_sem.at[p])
        for p, at in enumerate(stripes)
    ]
    for load in olds:
        load.start()
    others = [lax.rem(r + j, n) for j in range(1, n)]
    beside = [lax.rem(c + j, n) for j in range(1, n)]
    hail([(g, rr, c) for rr in others] + [(g, r, cc) for cc in beside])
    for load in loads[:3]:
        load.wait()
    blocks = m_ref.shape[1]
    width = tile // blocks
    for b in range(blocks):
        at = slice(b * width, (b + 1) * width)
        kept = m_ref[:, b : b + 1].astype(jnp.float32)
        diff[:, at] = (kept * w_ref[:, at] - d_ref[:, at]).astype(jnp.bfloat16)
    meet(len(others) + len(beside))

    root = r == c
    partner = c + 1 - 2 * lax.rem(c, 2)
    twins = [lax.rem(c + 2 * j, n) for j in range(1, n // 2)]
    even = lax.rem(r, 2) == lax.rem(c, 2)
    hops = [(k, sign) for k in range(max(n - 2, 1), 0, -1) for sign in (1, -1)]
    any_dev = (g, r, partner)

    def line(kind, src, panel, act):
        for i, (k, sign) in enumerate(hops):
            dest = r + sign * k
            copy = remote(src, panel.at[r], send_l.at[kind, i], recv_l.at[kind, r], (g, dest, c))

            @pl.when(jnp.logical_and(dest >= 0, dest < n))
            def _():
                act(copy)

    def got_line(kind, panel, s):
        remote(panel.at[s], panel.at[s], send_l.at[kind, 0], recv_l.at[kind, s], any_dev).wait_recv()

    def relay(kind, panel, act):
        if n == 2:
            return
        for at, s, dest in ((1, n - 1, 0), (n - 2, 0, n - 1)):
            copy = remote(panel.at[s], panel.at[s], relay_l.at[kind], recv_l.at[kind, s], (g, dest, c))

            @pl.when(r == at)
            def _():
                act(copy, s)

    def pass_on(kind, panel):
        def act(copy, s):
            got_line(kind, panel, s)
            copy.start()

        relay(kind, panel, act)

    def across(s, src, act):
        for i, cc in enumerate(twins + [partner]):
            act(remote(src, rowt.at[s], send_x.at[i, s], recv_x.at[s], (g, r, cc)))

    def down(s, act):
        act(remote(rowt.at[s], rowt.at[s], send_x.at[0, s], recv_x.at[s], any_dev))

    def got_x(s):
        down(s, lambda copy: copy.wait_recv())

    start = lambda copy: copy.start()
    sent = lambda copy: copy.wait_send()
    line(0, diff, cold, start)
    loads[3].wait()
    line(1, tok_ref, colp, start)

    @pl.when(root)
    def _():
        across(r, tok_ref, start)

    cold[r] = diff[...]
    colp[r] = tok_ref[...]
    total = jnp.zeros((held, width), jnp.float32)
    for b in range(blocks):
        value = tok_ref[:, b * width : (b + 1) * width].astype(jnp.float32)
        total = total + value * value
    total = jnp.sum(total.reshape(held // 8, 8, width), axis=0)
    tsum[...] = scaled(total, n * held)

    pass_on(0, cold)

    def near(s):
        if n == 2:
            return True
        far = jnp.logical_or(jnp.logical_and(r == 1, s == n - 1), jnp.logical_and(r == n - 2, s == 0))
        return jnp.logical_not(far)

    def got_panel(kind, panel, s):
        @pl.when(near(s))
        def _():
            got_line(kind, panel, s)

    for s in others:
        got_panel(0, cold, s)

    same = lax.broadcasted_iota(jnp.int32, (width, width), 0) == lax.broadcasted_iota(
        jnp.int32, (width, width), 1
    )

    def piece(p, cc, act):
        at = stripes[p]
        i = lax.rem(cc - c + n, n) - 1
        act(remote(
            pout.at[cc, :, at], pgot.at[c, :, at], send_p.at[p, i], recv_p.at[p, c], (g, r, cc)
        ))

    def multiply(p):
        at = stripes[p]
        olds[p].wait()
        value = lax.dot_general(
            old[at, :].astype(jnp.bfloat16), cold[...].reshape(n * depth, tile), (((1,), (1,)), ((), ())),
            preferred_element_type=jnp.float32,
        ).T.reshape(n, depth, span)
        part[:, :, at] = value
        pout[:, :, at] = value.astype(jnp.bfloat16)
        for cc in beside:
            piece(p, cc, start)

        @pl.when(root)
        def _():
            for b in range(p * span // width, (p + 1) * span // width):
                at = slice(b * width, (b + 1) * width)
                diag = jnp.where(same, old[at, at], 0.0)
                tsum[...] += jnp.sum(diag.reshape(width // 8, 8, width), axis=0)

    def owner(p):
        at = stripes[p]
        return remote(gred.at[:, at], gsum.at[:, at], send_f.at[p], recv_f.at[p], (g, c, r))

    def reduce(p):
        at = stripes[p]
        for cc in beside:
            remote(pout.at[cc, :, at], pgot.at[cc, :, at], send_p.at[p, 0], recv_p.at[p, cc], any_dev).wait_recv()
        value = part[c, :, at]
        for cc in beside:
            value = value + pgot[cc, :, at].astype(jnp.float32)
        gred[:, at] = value.astype(jnp.bfloat16)

        @pl.when(root)
        def _():
            gsum[:, at] = value.astype(jnp.bfloat16)

        @pl.when(jnp.logical_not(root))
        def _():
            owner(p).start()

    def spread_root(order):
        @pl.when(root)
        def _():
            for s in order:
                got_panel(1, colp, s)
                across(s, colp.at[s], start)

    def spread_twin(order):
        @pl.when(jnp.logical_and(even, jnp.logical_not(root)))
        def _():
            for s in order:
                got_x(s)
                down(s, start)

    multiply(0)
    pass_on(1, colp)
    for p in range(1, parts):
        multiply(p)
    spread_root(others)
    spread_twin([r] + others)
    trace_row = [remote(tsum, trow.at[c], send_t.at[i], recv_t.at[c], (g, r, cc)) for i, cc in enumerate(beside)]
    for copy in trace_row:
        copy.start()
    trow[c] = tsum[...]
    for p in range(parts - 1):
        reduce(p)

    @pl.when(jnp.logical_not(root))
    def _():
        for s in others:
            got_panel(1, colp, s)

    mine[...] = jnp.zeros_like(mine)
    mine[:, : n * held] = lax.dot_general(
        diff[...], colp[...].reshape(n * held, tile), (((1,), (1,)), ((), ())),
        preferred_element_type=jnp.float32,
    )
    cross = [remote(mine, mgot.at[c], send_m.at[i], recv_m.at[c], (g, r, cc)) for i, cc in enumerate(beside)]
    for copy in cross:
        copy.start()
    mgot[c] = mine[...]
    for cc in beside:
        remote(tsum, trow.at[cc], send_t.at[0], recv_t.at[cc], any_dev).wait_recv()
    total = jnp.zeros(tsum.shape, jnp.float32)
    for cc in range(n):
        total = total + trow[cc]
    tgot[r] = total
    trace_col = [remote(tgot.at[r], tgot.at[r], send_u.at[i], recv_u.at[r], (g, rr, c)) for i, rr in enumerate(others)]
    for copy in trace_col:
        copy.start()
    reduce(parts - 1)

    @pl.when(root)
    def _():
        for s in range(n):
            rowt[s] = colp[s]

    @pl.when(jnp.logical_not(jnp.logical_or(root, even)))
    def _():
        for s in range(n):
            got_x(s)

    for cc in beside:
        remote(mine, mgot.at[cc], send_m.at[0], recv_m.at[cc], any_dev).wait_recv()
    for rr in others:
        remote(tsum, tgot.at[rr], send_u.at[0], recv_u.at[rr], any_dev).wait_recv()

    @pl.when(jnp.logical_not(root))
    def _():
        for p in range(parts):
            owner(p).wait_recv()

    for kind, src, panel in ((0, diff, cold), (1, tok_ref, colp)):
        line(kind, src, panel, sent)
        relay(kind, panel, lambda copy, s: copy.wait_send())

    @pl.when(root)
    def _():
        across(r, tok_ref, sent)
        for s in others:
            across(s, colp.at[s], sent)

    @pl.when(jnp.logical_and(even, jnp.logical_not(root)))
    def _():
        for s in range(n):
            down(s, sent)

    for p in range(parts):
        for cc in beside:
            piece(p, cc, sent)

    @pl.when(jnp.logical_not(root))
    def _():
        for p in range(parts):
            owner(p).wait_send()

    for copy in trace_row + cross + trace_col:
        copy.wait_send()


def main_kernel(
    n, rows, old_ref, rt_ref, cp_ref, g_ref, mix_ref, trace_ref, w_ref, m_ref, out_hbm, new_hbm,
    out, new, out_sem, new_sem,
):
    tile = old_ref.shape[0]
    tokens = rt_ref.shape[0]
    steps = tile // rows
    slots = out.shape[0]

    def store(i):
        return pltpu.make_async_copy(
            out.at[lax.rem(i, slots)],
            out_hbm.at[pl.ds(pl.multiple_of(i * rows, rows), rows), :],
            out_sem.at[lax.rem(i, slots)],
        )

    @pl.loop(0, steps)
    def _(i):
        slot = lax.rem(i, slots)

        @pl.when(i >= slots)
        def _():
            store(i - slots).wait()

        here = pl.ds(pl.multiple_of(i * rows, rows), rows)
        gram = lax.dot_general(
            rt_ref[:, here], cp_ref[...], (((0,), (0,)), ((), ())), preferred_element_type=jnp.float32
        )
        out[slot] = old_ref[here, :] + scaled(gram, tokens)
        store(i).start()

    total = jnp.zeros(trace_ref.shape[1:], jnp.float32)
    for s in range(n):
        total = total + trace_ref[s]
    step = 0.25 * (tile * n) / jnp.sum(total, axis=(0, 1), keepdims=True)
    mix = jnp.zeros(mix_ref.shape[1:], jnp.float32)
    for s in range(n):
        mix = mix + mix_ref[s]
    mix = mix[:, :tokens]
    high = mix.astype(jnp.bfloat16)
    low = (mix - high.astype(jnp.float32)).astype(jnp.bfloat16)
    both = jnp.concatenate([high, low], axis=0)
    depth = high.shape[0]
    blocks = m_ref.shape[1]
    width = tile // blocks
    for b in range(blocks):
        at = slice(b * width, (b + 1) * width)
        extra = jnp.dot(both, cp_ref[:, at], preferred_element_type=jnp.float32)
        extra = scaled(extra[:depth] + extra[depth:], tokens)
        grad = g_ref[:, at].astype(jnp.float32) + extra
        kept = m_ref[:, b : b + 1].astype(jnp.float32)
        new[:, at] = kept * (w_ref[:, at] - step * grad)
    last = pltpu.make_async_copy(new, new_hbm, new_sem)
    last.start()
    for k in range(min(slots, steps)):
        store(jnp.int32(steps - 1 - k)).wait()
    last.wait()


def fused(n, hessian_old, tokens, weight, dense_weight, block_mask):
    tile = hessian_old.shape[0]
    held = tokens.shape[0]
    depth = weight.shape[0]
    vmem = pl.BlockSpec(memory_space=pltpu.VMEM)
    dma = pltpu.SemaphoreType.DMA
    hbm = pl.BlockSpec(memory_space=pltpu.HBM)
    parts = 3 if tile % 384 == 0 else 1
    wide = -(-n * held // 128) * 128
    old, colp, rowt, gsum, mix, trace = pl.pallas_call(
        functools.partial(exchange_kernel, n, parts),
        out_shape=(
            jax.ShapeDtypeStruct((tile, tile), jnp.float32),
            jax.ShapeDtypeStruct((n, held, tile), jnp.bfloat16),
            jax.ShapeDtypeStruct((n, held, tile), jnp.bfloat16),
            jax.ShapeDtypeStruct((depth, tile), jnp.bfloat16),
            jax.ShapeDtypeStruct((n, depth, wide), jnp.float32),
            jax.ShapeDtypeStruct((n, 8, 128), jnp.float32),
        ),
        in_specs=[hbm] * 5,
        out_specs=(vmem,) * 6,
        scratch_shapes=[
            pltpu.VMEM((held, tile), jnp.bfloat16),
            pltpu.VMEM((depth, tile), jnp.float32),
            pltpu.VMEM((depth, tile), jnp.float32),
            pltpu.VMEM(block_mask.shape, jnp.int32),
            pltpu.VMEM((depth, tile), jnp.bfloat16),
            pltpu.VMEM((n, depth, tile), jnp.bfloat16),
            pltpu.VMEM((n, depth, tile), jnp.float32),
            pltpu.VMEM((n, depth, tile), jnp.bfloat16),
            pltpu.VMEM((n, depth, tile), jnp.bfloat16),
            pltpu.VMEM((depth, tile), jnp.bfloat16),
            pltpu.VMEM((depth, wide), jnp.float32),
            pltpu.VMEM((n, 8, 128), jnp.float32),
            pltpu.VMEM((8, 128), jnp.float32),
            dma((4,)),
            dma((parts,)),
            dma((2, 2 * n)),
            dma((2, n)),
            dma((2,)),
            dma((n // 2, n)),
            dma((n,)),
            dma((parts, n)),
            dma((parts, n)),
            dma((parts,)),
            dma((parts,)),
            dma((n - 1,)),
            dma((n,)),
            dma((n - 1,)),
            dma((n,)),
            dma((n - 1,)),
            dma((n,)),
        ],
        compiler_params=pltpu.CompilerParams(
            collective_id=0, has_side_effects=True, vmem_limit_bytes=16 << 20
        ),
    )(*[pltpu.with_memory_space_constraint(x, pltpu.HBM) for x in (hessian_old, tokens, weight, dense_weight, block_mask)])
    colp = colp.reshape(n * held, tile)
    rowt = rowt.reshape(n * held, tile)
    rows = 256 if tile % 256 == 0 else 128
    hessian, new_weight = pl.pallas_call(
        functools.partial(main_kernel, n, rows),
        out_shape=(
            jax.ShapeDtypeStruct((tile, tile), jnp.float32),
            jax.ShapeDtypeStruct((depth, tile), jnp.float32),
        ),
        in_specs=[vmem] * 8,
        out_specs=(hbm, hbm),
        scratch_shapes=[
            pltpu.VMEM((3, rows, tile), jnp.float32),
            pltpu.VMEM((depth, tile), jnp.float32),
            dma((3,)),
            dma,
        ],
        compiler_params=pltpu.CompilerParams(vmem_limit_bytes=16 << 20),
    )(old, rowt, colp, gsum, mix, trace, weight, block_mask)
    return hessian, new_weight


def solution(mesh):
    n = mesh.shape["row"]

    def on_device(hessian_old, tokens, weight, dense_weight, block_mask):
        tile = hessian_old.shape[0]
        fits = (
            n == mesh.shape["col"]
            and n > 1
            and n % 2 == 0
            and tile == hessian_old.shape[1]
            and tile % 128 == 0
            and tile == block_mask.shape[1] * 128
            and tokens.shape[0] % 16 == 0
            and weight.shape[0] % 16 == 0
        )
        args = (hessian_old, tokens, weight, dense_weight, block_mask)
        return fused(n, *args) if fits else general(*args)

    spec = P(("grp", "row"), "col")
    return jax.shard_map(
        on_device, mesh=mesh, in_specs=(spec,) * 5, out_specs=(spec, spec), check_vma=False
    )
```

time: 39.6 us -> 41.8 us (1.056)
  Pallas kernels: 38.1 us -> 41 us
  local copies, waits for them, and re-layouts: 0.67 us -> 0.01 us
    pallas_call x3 -> x2, Pallas kernels: 38.1 us -> 41 us  [the longest x1 33.2 us: fused(): pl.pallas_call(functools.partial(exchange_kernel, n, parts), out_shape=(j...]
    unnamed x5 -> x4, local copies, waits for them, and re-layouts: 0.67 us -> 0.01 us
where the time goes in v1:
time: 41.8 us; the launch traced here: 41.7 us
  Pallas kernels  41 us (98%)
  between operations  0.67 us (2%)
    pallas_call x1, Pallas kernels, fused(): pl.pallas_call(functools.partial(exchange_kernel, n, parts), out_shape=(j...  33.2 us
    pallas_call x1, Pallas kernels, fused(): pl.pallas_call(functools.partial(main_kernel, n, rows), out_shape=(jax.Sh...  7.76 us

profile of v1, /device:TPU:0, one launch (start us, length us, event | category | flops | bytes accessed | tf_op | source)
XLA Modules:
  0.0 41.7 jit_solution(3159739838866589475)
XLA Ops:
  0.6 0.0 copy-start.1
  0.6 0.0 copy-start
  0.7 33.2 %shard_map.68 = (f32[2304,2304]{1,0:T(8,128)S(1)}, bf16[4,16,2304]{2,1,0:T(8,128)(2,1)S(1)}, bf16[4,16,2304]{2,1,0:T(8,128)(2,1)S(1)}, bf16[16,2304]{1,0:T(8,128...) custom-call(f32[2304,2304]{1,0:T(8,128)} %old_hbm.1, bf16[16,2304]{1,0:T(8,128)(2,1)} %tok_hbm.1, ...), custom_call_target="tpu_custom_call" | custom-call | tf_op jit(solution)/shard_map/pallas_call | solution.py:411
  33.9 0.0 copy-done.1
  33.9 0.0 copy-done
  33.9 7.8 %shard_map.69 = (f32[2304,2304]{1,0:T(8,128)}, f32[16,2304]{1,0:T(8,128)}) custom-call(f32[2304,2304]{1,0:T(8,128)S(1)} %get-tuple-element.8.old_ref, bf16[64,2304]{1,0:T(8,128)(2,1)S(1)} %bitcast.3, bf16[64,2304]{1,0:T(8,128)(2,1)S(1)} %bitcast.2, bf16[16,2304]{1,0:T(8,128)(2,1)S(1)} %get-tuple-element.11.g_ref, ...), custom_call_target="tpu_custom_call" | custom-call | tf_op jit(solution)/shard_map/pallas_call | solution.py:462
Async XLA Ops:
  0.6 33.3 %copy-start.1 = (s32[16,18]{1,0:T(8,128)S(1)}, s32[16,18]{1,0:T(8,128)}, u32[]{:S(2)}) copy-start(s32[16,18]{1,0:T(8,128)} %m_ref.1) | copy-start | bytes 3460
  0.6 33.3 %copy-start = (f32[16,2304]{1,0:T(8,128)S(1)}, f32[16,2304]{1,0:T(8,128)}, u32[]{:S(2)}) copy-start(f32[16,2304]{1,0:T(8,128)} %w_ref.1) | copy-start | bytes 442372

commit v2 on v0

v2 whole, which is shorter than its diff:
```python
import functools

import jax
import jax.numpy as jnp
from jax import lax
from jax.experimental import pallas as pl
from jax.experimental.pallas import tpu as pltpu
from jax.sharding import PartitionSpec as P

MESH = pl.DeviceIdType.MESH


def general(hessian_old, tokens, weight, dense_weight, block_mask):
    row_tile = hessian_old.shape[0]
    col_tile = hessian_old.shape[1]
    row_idx = lax.axis_index("row")
    col_idx = lax.axis_index("col")
    col_panel = lax.all_gather(tokens, "row", axis=0, tiled=True)
    features = lax.all_gather(tokens, "col", axis=1, tiled=True)
    row_panel = lax.all_to_all(features, "row", split_axis=1, concat_axis=0, tiled=True)
    gram_tile = lax.dot_general(
        row_panel, col_panel, (((0,), (0,)), ((), ())), preferred_element_type=jnp.float32
    )
    token_count = tokens.shape[0] * lax.axis_size("row")
    hessian = hessian_old + gram_tile / token_count
    row_ids = lax.broadcasted_iota(jnp.int32, (row_tile, col_tile), 0) + row_idx * row_tile
    col_ids = lax.broadcasted_iota(jnp.int32, (row_tile, col_tile), 1) + col_idx * col_tile
    local_trace = jnp.sum(jnp.where(row_ids == col_ids, hessian, jnp.float32(0.0)))
    diag_sum = lax.psum(local_trace, ("row", "col"))
    weight_rows = weight.shape[0]
    block_count = block_mask.shape[1]
    block_width = col_tile // block_count
    kept_mask = (
        block_mask.astype(jnp.float32)[:, :, None] * jnp.ones((1, 1, block_width), jnp.float32)
    ).reshape(weight_rows, col_tile)
    difference = (kept_mask * weight - dense_weight).astype(jnp.bfloat16)
    hess_low = hessian.astype(jnp.bfloat16)
    partial_grad = lax.dot_general(
        lax.all_gather(difference, "row", axis=0, tiled=True),
        hess_low,
        (((1,), (1,)), ((), ())),
        preferred_element_type=jnp.float32,
    )
    spread = lax.all_to_all(partial_grad, "row", split_axis=0, concat_axis=1, tiled=True)
    gradient = lax.psum_scatter(spread, "col", scatter_dimension=1, tiled=True)
    step_size = 0.25 * (row_tile * lax.axis_size("row")) / diag_sum
    new_weight = kept_mask * (weight - step_size * gradient)
    return (hessian, new_weight)


def hail(devices):
    barrier = pltpu.get_barrier_semaphore()
    for device in devices:
        pl.semaphore_signal(barrier, inc=1, device_id=device, device_id_type=MESH)


def meet(count):
    pl.semaphore_wait(pltpu.get_barrier_semaphore(), count)


def remote(src, dst, send_sem, recv_sem, device):
    return pltpu.make_async_remote_copy(
        src_ref=src, dst_ref=dst, send_sem=send_sem, recv_sem=recv_sem,
        device_id=device, device_id_type=MESH,
    )


def scaled(value, count):
    exact = count & (count - 1) == 0
    return value * (1.0 / count) if exact else value / count


def split(value):
    high = value.astype(jnp.bfloat16)
    return high, value - high.astype(jnp.float32)


def gather_kernel(
    n, parts, old_hbm, tok_hbm, w_hbm, d_hbm, m_hbm, old, colp, rowt, *refs
):
    outs, refs = refs[:n], refs[n:]
    (
        tok_ref, w_ref, d_ref, m_ref, diff, rowd, dsum, pack,
        in_sem, old_sem, send_a, recv_a, send_r, send_d, recv_d, send_x, recv_x, send_s, recv_s,
    ) = refs
    g, r, c = lax.axis_index("grp"), lax.axis_index("row"), lax.axis_index("col")
    tile = old.shape[0]
    held = tok_ref.shape[0]
    depth = diff.shape[0]
    loads = [
        pltpu.make_async_copy(src, dst, in_sem.at[i])
        for i, (src, dst) in enumerate([(w_hbm, w_ref), (d_hbm, d_ref), (m_hbm, m_ref), (tok_hbm, tok_ref)])
    ]
    for load in loads:
        load.start()
    others = [lax.rem(r + j, n) for j in range(1, n)]
    beside = [lax.rem(c + j, n) for j in range(1, n)]
    hail([(g, rr, c) for rr in others] + [(g, r, cc) for cc in beside])
    for load in loads:
        load.wait()
    whole = pltpu.make_async_copy(old_hbm, old, old_sem)
    whole.start()
    blocks = m_ref.shape[1]
    width = tile // blocks
    for b in range(blocks):
        at = slice(b * width, (b + 1) * width)
        kept = m_ref[:, b : b + 1].astype(jnp.float32)
        diff[:, at] = (kept * w_ref[:, at] - d_ref[:, at]).astype(jnp.bfloat16)
    meet(len(others) + len(beside))

    root = r == c
    partner = c + 1 - 2 * lax.rem(c, 2)
    partner_dev = (g, r, partner)
    twins = [lax.rem(c + 2 * j, n) for j in range(1, n // 2)]
    even = lax.rem(r, 2) == lax.rem(c, 2)
    twin = jnp.logical_and(even, jnp.logical_not(root))
    mate = partner
    crosses = r // 2 != c // 2
    panels = (rowd, rowt)
    sources = (diff, tok_ref)
    start = lambda copy: copy.start()
    sent = lambda copy: copy.wait_send()

    def direct(rr):
        return jnp.logical_and(rr != r, jnp.logical_not(jnp.logical_and(crosses, rr == mate)))

    def relay(s, act):
        copy = remote(colp.at[s], colp.at[s], send_r.at[s], recv_a.at[s], (g, mate, c))

        @pl.when(s // 2 != r // 2)
        def _():
            act(copy)

    def token_copy(k):
        rr = lax.rem(c + k, n)
        return rr, remote(tok_ref, colp.at[r], send_a.at[k], recv_a.at[r], (g, rr, c))

    diff_copy = remote(diff, rowd.at[r], send_d, recv_d.at[r], (g, c, c))

    def spread(kind, s, src, act):
        for i, cc in enumerate(twins + [partner]):
            act(remote(src, panels[kind].at[s], send_x.at[i, kind, s], recv_x.at[kind, s], (g, r, cc)))

    def spread_on(kind, s, act):
        at = panels[kind].at[s]
        act(remote(at, at, send_x.at[0, kind, s], recv_x.at[kind, s], partner_dev))

    def got_a(s):
        remote(tok_ref, colp.at[s], send_a.at[0], recv_a.at[s], partner_dev).wait_recv()

    def got_x(kind, s):
        spread_on(kind, s, lambda copy: copy.wait_recv())

    def got_diff(s):
        remote(diff, rowd.at[s], send_d, recv_d.at[s], partner_dev).wait_recv()

    @pl.when(jnp.logical_not(root))
    def _():
        diff_copy.start()
        token_copy(0)[1].start()

    @pl.when(root)
    def _():
        spread(0, r, diff, start)
        spread(1, r, tok_ref, start)

    for k in range(1, n):
        rr, copy = token_copy(k)

        @pl.when(direct(rr))
        def _():
            copy.start()

    colp[r] = tok_ref[...]

    @pl.when(root)
    def _():
        rowd[r] = diff[...]
        for s in others:
            got_diff(s)
            spread(0, s, rowd.at[s], start)

    @pl.when(twin)
    def _():
        for s in [r] + others:
            got_x(0, s)
            spread_on(0, s, start)

    @pl.when(jnp.logical_not(even))
    def _():
        for s in range(n):
            got_x(0, s)

    same = lax.broadcasted_iota(jnp.int32, (width, width), 0) == lax.broadcasted_iota(
        jnp.int32, (width, width), 1
    )

    def diag_to(i, cc):
        return remote(dsum.at[0], dsum.at[1], send_s.at[i], recv_s, (g, r, cc))

    def tokens_step(i):
        s = others[i]

        @pl.when(root)
        def _():
            got_a(s)
            spread(1, s, colp.at[s], start)
            relay(s, start)

        @pl.when(twin)
        def _():
            q = ([r] + others)[i]
            got_x(1, q)
            spread_on(1, q, start)

    whole.wait()
    span = tile // parts
    for p in range(parts):
        at = slice(p * span, (p + 1) * span)
        value = jnp.dot(
            rowd[...].reshape(n * depth, tile), old[:, at].astype(jnp.bfloat16), preferred_element_type=jnp.float32
        )
        pack[:, :, at] = value.astype(jnp.bfloat16).reshape(n, depth, span)
        if p < n - 1:
            tokens_step(p)
    for i in range(parts, n - 1):
        tokens_step(i)

    @pl.when(twin)
    def _():
        got_x(1, others[-1])
        spread_on(1, others[-1], start)

    @pl.when(root)
    def _():
        total = jnp.zeros((8, width), jnp.float32)
        for b in range(blocks):
            at = slice(b * width, (b + 1) * width)
            diag = jnp.where(same, old[at, at], 0.0)
            total = total + jnp.sum(diag.reshape(width // 8, 8, width), axis=0)
        dsum[0] = total
        dsum[1] = total
        for i, cc in enumerate(beside):
            diag_to(i, cc).start()
        for s in range(n):
            rowt[s] = colp[s]

    @pl.when(jnp.logical_not(even))
    def _():
        for s in range(n):
            got_x(1, s)

    mix = lax.dot_general(
        rowd[...].reshape(n * depth, tile), rowt[...].reshape(n * held, tile), (((1,), (1,)), ((), ())),
        preferred_element_type=jnp.float32,
    )
    high, low = split(mix)
    pack[:, :, tile : tile + 2 * n * held] = jnp.concatenate(
        [high.astype(jnp.float32), low], axis=1
    ).astype(jnp.bfloat16).reshape(n, depth, 2 * n * held)
    total = jnp.zeros((n * held, width), jnp.float32)
    for b in range(blocks):
        value = rowt[:, :, b * width : (b + 1) * width].reshape(n * held, width).astype(jnp.float32)
        total = total + value * value
    total = scaled(jnp.sum(total.reshape(n * held // 8, 8, width), axis=0), n * held)

    @pl.when(jnp.logical_not(root))
    def _():
        diag_to(0, partner).wait_recv()

    high, low = split(total + dsum[1])
    both = jnp.concatenate([high.astype(jnp.float32), low], axis=0).astype(jnp.bfloat16)
    for s in range(n):
        pack[s, :, tile + 2 * n * held :] = both
    for k in range(n):
        outs[k][...] = pack[lax.rem(r + k, n)]

    @pl.when(jnp.logical_not(root))
    def _():
        for s in others:
            got_a(s)
        diff_copy.wait_send()
        token_copy(0)[1].wait_send()

    @pl.when(root)
    def _():
        spread(0, r, diff, sent)
        spread(1, r, tok_ref, sent)
        for s in others:
            spread(0, s, rowd.at[s], sent)
            spread(1, s, colp.at[s], sent)
            relay(s, sent)
        for i, cc in enumerate(beside):
            diag_to(i, cc).wait_send()

    @pl.when(twin)
    def _():
        for kind in (0, 1):
            for s in range(n):
                spread_on(kind, s, sent)

    for k in range(1, n):
        rr, copy = token_copy(k)

        @pl.when(direct(rr))
        def _():
            copy.wait_send()


def main_kernel(rows, old_ref, rt_ref, cp_ref, out_hbm, out, out_sem):
    tile = old_ref.shape[0]
    tokens = rt_ref.shape[0]
    steps = tile // rows
    slots = out.shape[0]

    def store(i):
        return pltpu.make_async_copy(
            out.at[lax.rem(i, slots)],
            out_hbm.at[pl.ds(pl.multiple_of(i * rows, rows), rows), :],
            out_sem.at[lax.rem(i, slots)],
        )

    @pl.loop(0, steps)
    def _(i):
        slot = lax.rem(i, slots)

        @pl.when(i >= slots)
        def _():
            store(i - slots).wait()

        here = pl.ds(pl.multiple_of(i * rows, rows), rows)
        gram = lax.dot_general(
            rt_ref[:, here], cp_ref[...], (((0,), (0,)), ((), ())), preferred_element_type=jnp.float32
        )
        out[slot] = old_ref[here, :] + scaled(gram, tokens)
        store(i).start()

    for k in range(min(slots, steps)):
        store(jnp.int32(steps - 1 - k)).wait()


def step_kernel(n, *refs):
    got, (cp_ref, w_ref, m_ref, new_hbm, new, new_sem) = refs[:n], refs[n:]
    depth, tile = w_ref.shape
    tokens = cp_ref.shape[0]
    extra = got[0][:, tile:].astype(jnp.float32)
    for s in range(1, n):
        extra = extra + got[s][:, tile:].astype(jnp.float32)
    step = 0.25 * (tile * n) / jnp.sum(extra[:, 2 * tokens :], axis=(0, 1), keepdims=True)
    high, low = split(extra[:, :tokens] + extra[:, tokens : 2 * tokens])
    both = jnp.concatenate([high, low.astype(jnp.bfloat16)], axis=0)
    blocks = m_ref.shape[1]
    width = tile // blocks
    for b in range(blocks):
        at = slice(b * width, (b + 1) * width)
        value = jnp.dot(both, cp_ref[:, at], preferred_element_type=jnp.float32)
        grad = scaled(value[:depth] + value[depth:], tokens)
        for s in range(n):
            grad = grad + got[s][:, at].astype(jnp.float32)
        kept = m_ref[:, b : b + 1].astype(jnp.float32)
        new[:, at] = kept * (w_ref[:, at] - step * grad)
    last = pltpu.make_async_copy(new, new_hbm, new_sem)
    last.start()
    last.wait()


def fused(n, hessian_old, tokens, weight, dense_weight, block_mask):
    tile = hessian_old.shape[0]
    held = tokens.shape[0]
    depth = weight.shape[0]
    vmem = pl.BlockSpec(memory_space=pltpu.VMEM)
    dma = pltpu.SemaphoreType.DMA
    hbm = pl.BlockSpec(memory_space=pltpu.HBM)
    parts = 3 if tile % 384 == 0 else 1
    wide = tile + 2 * n * held + 128
    old, colp, rowt, *packs = pl.pallas_call(
        functools.partial(gather_kernel, n, parts),
        out_shape=(
            jax.ShapeDtypeStruct((tile, tile), jnp.float32),
            jax.ShapeDtypeStruct((n, held, tile), jnp.bfloat16),
            jax.ShapeDtypeStruct((n, held, tile), jnp.bfloat16),
        )
        + (jax.ShapeDtypeStruct((depth, wide), jnp.bfloat16),) * n,
        in_specs=[hbm] * 5,
        out_specs=(vmem,) * (3 + n),
        scratch_shapes=[
            pltpu.VMEM((held, tile), jnp.bfloat16),
            pltpu.VMEM((depth, tile), jnp.float32),
            pltpu.VMEM((depth, tile), jnp.float32),
            pltpu.VMEM(block_mask.shape, jnp.int32),
            pltpu.VMEM((depth, tile), jnp.bfloat16),
            pltpu.VMEM((n, depth, tile), jnp.bfloat16),
            pltpu.VMEM((2, 8, 128), jnp.float32),
            pltpu.VMEM((n, depth, wide), jnp.bfloat16),
            dma((4,)),
            dma,
            dma((n,)),
            dma((n,)),
            dma((n,)),
            dma,
            dma((n,)),
            dma((n // 2, 2, n)),
            dma((2, n)),
            dma((n - 1,)),
            dma,
        ],
        compiler_params=pltpu.CompilerParams(
            collective_id=0, has_side_effects=True, vmem_limit_bytes=16 << 20
        ),
    )(*[pltpu.with_memory_space_constraint(x, pltpu.HBM) for x in (hessian_old, tokens, weight, dense_weight, block_mask)])
    colp = colp.reshape(n * held, tile)
    rowt = rowt.reshape(n * held, tile)
    got = [packs[0]] + [
        lax.ppermute(packs[k], "row", [(i, (i + k) % n) for i in range(n)]) for k in range(1, n)
    ]
    rows = 256 if tile % 256 == 0 else 128
    hessian = pl.pallas_call(
        functools.partial(main_kernel, rows),
        out_shape=jax.ShapeDtypeStruct((tile, tile), jnp.float32),
        in_specs=[vmem] * 3,
        out_specs=hbm,
        scratch_shapes=[pltpu.VMEM((3, rows, tile), jnp.float32), dma((3,))],
        compiler_params=pltpu.CompilerParams(vmem_limit_bytes=12 << 20),
        cost_estimate=pl.CostEstimate(
            flops=2 * n * held * tile * tile, bytes_accessed=8 * tile * tile, transcendentals=0
        ),
    )(old, rowt, colp)
    new_weight = pl.pallas_call(
        functools.partial(step_kernel, n),
        out_shape=jax.ShapeDtypeStruct((depth, tile), jnp.float32),
        in_specs=[vmem] * (n + 3),
        out_specs=hbm,
        scratch_shapes=[pltpu.VMEM((depth, tile), jnp.float32), dma],
        compiler_params=pltpu.CompilerParams(vmem_limit_bytes=4 << 20),
    )(*got, colp, weight, block_mask)
    return hessian, new_weight


def solution(mesh):
    n = mesh.shape["row"]

    def on_device(hessian_old, tokens, weight, dense_weight, block_mask):
        tile = hessian_old.shape[0]
        fits = (
            n == mesh.shape["col"]
            and n > 1
            and n % 2 == 0
            and tile == hessian_old.shape[1]
            and tile % 128 == 0
            and tile == block_mask.shape[1] * 128
            and tokens.shape[0] % 16 == 0
            and weight.shape[0] == 16
            and tokens.shape[0] * n % 64 == 0
        )
        args = (hessian_old, tokens, weight, dense_weight, block_mask)
        return fused(n, *args) if fits else general(*args)

    spec = P(("grp", "row"), "col")
    return jax.shard_map(
        on_device, mesh=mesh, in_specs=(spec,) * 5, out_specs=(spec, spec), check_vma=False
    )
```

time: 39.6 us -> 33.6 us (0.85)
  Pallas kernels: 38.1 us -> 26.3 us
  starting transfers between devices: 0 us -> 6.46 us
  local copies, waits for them, and re-layouts: 0.67 us -> 0.01 us
    pallas_call x3, Pallas kernels: 38.1 us -> 26.3 us  [the longest x1 17.6 us: fused(): pl.pallas_call(functools.partial(gather_kernel, n, parts), out_shape=(jax...]
    ppermute x0 -> x3, starting transfers between devices: none -> 6.46 us  [fused(): lax.ppermute(packs[k], 'row', [(i, (i + k) % n) for i in range(n)])]
    unnamed x5 -> x4, local copies, waits for them, and re-layouts: 0.67 us -> 0.01 us
  transfers between devices with their start and end apart: 0 -> 3, of which waited for: 0 -> 0; matrix products, arithmetic and copies ran while one was open for 0% -> 0% of each run, Pallas kernels for 0% -> 23%
where the time goes in v2:
time: 33.6 us; the launch traced here: 33.4 us
  Pallas kernels  26.3 us (78%)
  starting transfers between devices  6.46 us (19%)
  between operations  0.69 us (2%)
    pallas_call x1, Pallas kernels, fused(): pl.pallas_call(functools.partial(gather_kernel, n, parts), out_shape=(jax...  17.6 us
    pallas_call x1, Pallas kernels, fused(): pl.pallas_call(functools.partial(main_kernel, rows), out_shape=jax.ShapeD...  7.73 us
    ppermute x3, starting transfers between devices, fused(): lax.ppermute(packs[k], 'row', [(i, (i + k) % n) for i in range(n)])  6.46 us
    pallas_call x1, Pallas kernels, fused(): pl.pallas_call(functools.partial(step_kernel, n), out_shape=jax.ShapeDtyp...  0.96 us
  transfers between devices with their start and end apart: 3, of which 0 were waited for; matrix products, arithmetic and copies ran while one was open for 0% of the time, Pallas kernels for 23%

profile of v2, /device:TPU:0, one launch (start us, length us, event | category | flops | bytes accessed | tf_op | source)
XLA Modules:
  0.0 33.4 jit_solution(12834904810696588319)
XLA Ops:
  0.6 17.6 %shard_map.68 = (f32[2304,2304]{1,0:T(8,128)S(1)}, bf16[4,16,2304]{2,1,0:T(8,128)(2,1)S(1)}, bf16[4,16,2304]{2,1,0:T(8,128)(2,1)S(1)}, bf16[16,2560]{1,0:T(8,128...) custom-call(f32[2304,2304]{1,0:T(8,128)} %old_hbm.1, ...), custom_call_target="tpu_custom_call" | custom-call | tf_op jit(solution)/shard_map/pallas_call | solution.py:376
  18.2 1.9 %collective-permute-start = (bf16[16,2560]{1,0:T(8,128)(2,1)S(1)}, bf16[16,2560]{1,0:T(8,128)(2,1)S(1)}, u32[]{:S(2)}, u32[]{:S(2)}) collective-permute-start(bf16[16,2560]{1,0:T(8,128)(2,1)S(1)} %get-tuple-element.13), channel_id=1, source_target_pairs={{0,4},{4,8},{8,12},{12,0},{1,5},{5,9},{9,13},{13,1},{2,6},{6,10},{... | collective-permute-start | bytes 245768 | tf_op jit(solution)/shard_map/ppermute | solution.py:414
  20.1 1.7 %collective-permute-start.1 = (bf16[16,2560]{1,0:T(8,128)(2,1)S(1)}, bf16[16,2560]{1,0:T(8,128)(2,1)S(1)}, u32[]{:S(2)}, u32[]{:S(2)}) collective-permute-start(bf16[16,2560]{1,0:T(8,128)(2,1)S(1)} %get-tuple-element.14), channel_id=1, source_target_pairs={{0,8},{4,12},{8,0},{12,4},{1,9},{5,13},{9,1},{13,5},{2,10},{6,14},... | collective-permute-start | bytes 245768 | tf_op jit(solution)/shard_map/ppermute | solution.py:414
  21.8 2.8 %collective-permute-start.2 = (bf16[16,2560]{1,0:T(8,128)(2,1)S(1)}, bf16[16,2560]{1,0:T(8,128)(2,1)S(1)}, u32[]{:S(2)}, u32[]{:S(2)}) collective-permute-start(bf16[16,2560]{1,0:T(8,128)(2,1)S(1)} %get-tuple-element.15), channel_id=1, source_target_pairs={{0,12},{4,0},{8,4},{12,8},{1,13},{5,1},{9,5},{13,9},{2,14},{6,2},{... | collective-permute-start | bytes 245768 | tf_op jit(solution)/shard_map/ppermute | solution.py:414
  24.7 0.0 copy-start
  24.7 0.0 copy-start.1
  24.7 7.7 %shard_map.69 = f32[2304,2304]{1,0:T(8,128)} custom-call(f32[2304,2304]{1,0:T(8,128)S(1)} %get-tuple-element.9.old_ref, bf16[64,2304]{1,0:T(8,128)(2,1)S(1)} %bitcast.4, bf16[64,2304]{1,0:T(8,128)(2,1)S(1)} %bitcast.2), custom_call_target="tpu_custom_call" | custom-call | flops 679477248 | bytes 42467328 | tf_op jit(solution)/shard_map/pallas_call | solution.py:417
  32.4 0.0 collective-permute-done.refs_1_
  32.4 0.0 collective-permute-done.1.refs_2_
  32.4 0.0 collective-permute-done.2.refs_3_
  32.4 0.0 copy-done
  32.4 0.0 copy-done.1
  32.5 1.0 %shard_map.70 = f32[16,2304]{1,0:T(8,128)} custom-call(bf16[16,2560]{1,0:T(8,128)(2,1)S(1)} %get-tuple-element.12.refs_0_, bf16[16,2560]{1,0:T(8,128)(2,1)S(1)} %collective-permute-done.refs_1_, bf16[16,2560]{1,0:T(8,128)(2,1)S(1)} %collective-permute-done.1.refs_2_, bf16[16,2560]{1,0:T(8,128)(2,1)S(1)} %collective-permute-done.2.refs_3_, ...), custom_call_target="tpu_custom_call" | custom-call | tf_op jit(solution)/shard_map/pallas_call | solution.py:428
Async XLA Ops:
  18.2 14.2 %collective-permute-start = (bf16[16,2560]{1,0:T(8,128)(2,1)S(1)}, bf16[16,2560]{1,0:T(8,128)(2,1)S(1)}, u32[]{:S(2)}, u32[]{:S(2)}) collective-permute-start(bf16[16,2560]{1,0:T(8,128)(2,1)S(1)} %get-tuple-element.13), channel_id=1, source_target_pairs={{0,4},{4,8},{8,12},{12,0},{1,5},{5,9},{9,13},{13,1},{2,6},{6,10},{... | collective-permute-start | bytes 245768 | tf_op jit(solution)/shard_map/ppermute | solution.py:414
  20.1 12.3 %collective-permute-start.1 = (bf16[16,2560]{1,0:T(8,128)(2,1)S(1)}, bf16[16,2560]{1,0:T(8,128)(2,1)S(1)}, u32[]{:S(2)}, u32[]{:S(2)}) collective-permute-start(bf16[16,2560]{1,0:T(8,128)(2,1)S(1)} %get-tuple-element.14), channel_id=1, source_target_pairs={{0,8},{4,12},{8,0},{12,4},{1,9},{5,13},{9,1},{13,5},{2,10},{6,14},... | collective-permute-start | bytes 245768 | tf_op jit(solution)/shard_map/ppermute | solution.py:414
  21.8 10.6 %collective-permute-start.2 = (bf16[16,2560]{1,0:T(8,128)(2,1)S(1)}, bf16[16,2560]{1,0:T(8,128)(2,1)S(1)}, u32[]{:S(2)}, u32[]{:S(2)}) collective-permute-start(bf16[16,2560]{1,0:T(8,128)(2,1)S(1)} %get-tuple-element.15), channel_id=1, source_target_pairs={{0,12},{4,0},{8,4},{12,8},{1,13},{5,1},{9,5},{13,9},{2,14},{6,2},{... | collective-permute-start | bytes 245768 | tf_op jit(solution)/shard_map/ppermute | solution.py:414
  24.7 7.8 %copy-start = (f32[16,2304]{1,0:T(8,128)S(1)}, f32[16,2304]{1,0:T(8,128)}, u32[]{:S(2)}) copy-start(f32[16,2304]{1,0:T(8,128)} %refs_5_.1) | copy-start | bytes 442372
  24.7 7.8 %copy-start.1 = (s32[16,18]{1,0:T(8,128)S(1)}, s32[16,18]{1,0:T(8,128)}, u32[]{:S(2)}) copy-start(s32[16,18]{1,0:T(8,128)} %refs_6_.1) | copy-start | bytes 3460

commit v3 on v2

--- a/solution.py
+++ b/solution.py
@@ -73,6 +73,15 @@
 def split(value):
     high = value.astype(jnp.bfloat16)
     return high, value - high.astype(jnp.float32)
+
+
+def swap(index, mask):
+    bit = 1
+    while bit <= mask:
+        if mask & bit:
+            index = index + bit - 2 * bit * ((index // bit) % 2)
+        bit *= 2
+    return index
 
 
 def gather_kernel(
@@ -154,22 +163,30 @@
     def got_diff(s):
         remote(diff, rowd.at[s], send_d, recv_d.at[s], partner_dev).wait_recv()
 
+    late = lax.rem(c, 2) == 1
+
+    def tokens_out(first):
+        if first:
+            token_copy(0)[1].start()
+        for k in range(1, n):
+            rr, copy = token_copy(k)
+
+            @pl.when(direct(rr))
+            def _():
+                copy.start()
+
     @pl.when(jnp.logical_not(root))
     def _():
         diff_copy.start()
-        token_copy(0)[1].start()
+
+        @pl.when(jnp.logical_not(late))
+        def _():
+            tokens_out(True)
 
     @pl.when(root)
     def _():
         spread(0, r, diff, start)
         spread(1, r, tok_ref, start)
-
-    for k in range(1, n):
-        rr, copy = token_copy(k)
-
-        @pl.when(direct(rr))
-        def _():
-            copy.start()
 
     colp[r] = tok_ref[...]
 
@@ -180,16 +197,28 @@
             got_diff(s)
             spread(0, s, rowd.at[s], start)
 
+    @pl.when(root)
+    def _():
+        tokens_out(False)
+
     @pl.when(twin)
     def _():
-        for s in [r] + others:
+        for i, s in enumerate([r] + others):
             got_x(0, s)
             spread_on(0, s, start)
+            if i == 0:
+                @pl.when(late)
+                def _():
+                    tokens_out(True)
 
     @pl.when(jnp.logical_not(even))
     def _():
-        for s in range(n):
+        for i, s in enumerate([r] + others):
             got_x(0, s)
+            if i == 0:
+                @pl.when(late)
+                def _():
+                    tokens_out(True)
 
     same = lax.broadcasted_iota(jnp.int32, (width, width), 0) == lax.broadcasted_iota(
         jnp.int32, (width, width), 1
@@ -273,7 +302,7 @@
     for s in range(n):
         pack[s, :, tile + 2 * n * held :] = both
     for k in range(n):
-        outs[k][...] = pack[lax.rem(r + k, n)]
+        outs[k][...] = pack[swap(r, k)]
 
     @pl.when(jnp.logical_not(root))
     def _():
@@ -411,7 +440,7 @@
     colp = colp.reshape(n * held, tile)
     rowt = rowt.reshape(n * held, tile)
     got = [packs[0]] + [
-        lax.ppermute(packs[k], "row", [(i, (i + k) % n) for i in range(n)]) for k in range(1, n)
+        lax.ppermute(packs[k], "row", [(i, swap(i, k)) for i in range(n)]) for k in range(1, n)
     ]
     rows = 256 if tile % 256 == 0 else 128
     hessian = pl.pallas_call(
@@ -444,7 +473,7 @@
         fits = (
             n == mesh.shape["col"]
             and n > 1
-            and n % 2 == 0
+            and n & (n - 1) == 0
             and tile == hessian_old.shape[1]
             and tile % 128 == 0
             and tile == block_mask.shape[1] * 128

time: 33.6 us -> 31.4 us (0.935)
  starting transfers between devices: 6.46 us -> 5.09 us
  Pallas kernels: 26.3 us -> 25.2 us
    ppermute x3, starting transfers between devices: 6.46 us -> 5.09 us  [fused(): lax.ppermute(packs[k], 'row', [(i, swap(i, k)) for i in range(n)])]
    pallas_call x1, Pallas kernels: 17.6 us -> 16.5 us  [fused(): pl.pallas_call(functools.partial(gather_kernel, n, parts), out_shape=(jax...]
  transfers between devices with their start and end apart: 3 -> 3, of which waited for: 0 -> 0; matrix products, arithmetic and copies ran while one was open for 0% -> 0% of each run, Pallas kernels for 23% -> 25%
where the time goes in v3:
time: 31.4 us; the launch traced here: 31 us
  Pallas kernels  25.2 us (80%)
  starting transfers between devices  5.09 us (16%)
  between operations  0.69 us (2%)
    pallas_call x1, Pallas kernels, fused(): pl.pallas_call(functools.partial(gather_kernel, n, parts), out_shape=(jax...  16.5 us
    pallas_call x1, Pallas kernels, fused(): pl.pallas_call(functools.partial(main_kernel, rows), out_shape=jax.ShapeD...  7.74 us
    ppermute x3, starting transfers between devices, fused(): lax.ppermute(packs[k], 'row', [(i, swap(i, k)) for i in range(n)])  5.09 us
    pallas_call x1, Pallas kernels, fused(): pl.pallas_call(functools.partial(step_kernel, n), out_shape=jax.ShapeDtyp...  0.96 us
  transfers between devices with their start and end apart: 3, of which 0 were waited for; matrix products, arithmetic and copies ran while one was open for 0% of the time, Pallas kernels for 25%

profile of v3, /device:TPU:0, one launch (start us, length us, event | category | flops | bytes accessed | tf_op | source)
XLA Modules:
  0.0 31.0 jit_solution(18348196766302991343)
XLA Ops:
  0.6 16.5 %shard_map.68 = (f32[2304,2304]{1,0:T(8,128)S(1)}, bf16[4,16,2304]{2,1,0:T(8,128)(2,1)S(1)}, bf16[4,16,2304]{2,1,0:T(8,128)(2,1)S(1)}, bf16[16,2560]{1,0:T(8,128...) custom-call(f32[2304,2304]{1,0:T(8,128)} %old_hbm.1, ...), custom_call_target="tpu_custom_call" | custom-call | tf_op jit(solution)/shard_map/pallas_call | solution.py:405
  17.2 2.4 %collective-permute-start = (bf16[16,2560]{1,0:T(8,128)(2,1)S(1)}, bf16[16,2560]{1,0:T(8,128)(2,1)S(1)}, u32[]{:S(2)}, u32[]{:S(2)}) collective-permute-start(bf16[16,2560]{1,0:T(8,128)(2,1)S(1)} %get-tuple-element.13), channel_id=1, source_target_pairs={{0,4},{4,0},{8,12},{12,8},{1,5},{5,1},{9,13},{13,9},{2,6},{6,2},{1... | collective-permute-start | bytes 245768 | tf_op jit(solution)/shard_map/ppermute | solution.py:443
  19.6 2.6 %collective-permute-start.1 = (bf16[16,2560]{1,0:T(8,128)(2,1)S(1)}, bf16[16,2560]{1,0:T(8,128)(2,1)S(1)}, u32[]{:S(2)}, u32[]{:S(2)}) collective-permute-start(bf16[16,2560]{1,0:T(8,128)(2,1)S(1)} %get-tuple-element.14), channel_id=1, source_target_pairs={{0,8},{4,12},{8,0},{12,4},{1,9},{5,13},{9,1},{13,5},{2,10},{6,14},... | collective-permute-start | bytes 245768 | tf_op jit(solution)/shard_map/ppermute | solution.py:443
  22.3 0.0 collective-permute-start.2
  22.3 0.0 copy-start
  22.3 0.0 copy-start.1
  22.3 7.7 %shard_map.69 = f32[2304,2304]{1,0:T(8,128)} custom-call(f32[2304,2304]{1,0:T(8,128)S(1)} %get-tuple-element.9.old_ref, bf16[64,2304]{1,0:T(8,128)(2,1)S(1)} %bitcast.4, bf16[64,2304]{1,0:T(8,128)(2,1)S(1)} %bitcast.2), custom_call_target="tpu_custom_call" | custom-call | flops 679477248 | bytes 42467328 | tf_op jit(solution)/shard_map/pallas_call | solution.py:446
  30.0 0.0 collective-permute-done.refs_1_
  30.0 0.0 collective-permute-done.1.refs_2_
  30.0 0.0 collective-permute-done.2.refs_3_
  30.0 0.0 copy-done
  30.1 0.0 copy-done.1
  30.1 1.0 %shard_map.70 = f32[16,2304]{1,0:T(8,128)} custom-call(bf16[16,2560]{1,0:T(8,128)(2,1)S(1)} %get-tuple-element.12.refs_0_, bf16[16,2560]{1,0:T(8,128)(2,1)S(1)} %collective-permute-done.refs_1_, bf16[16,2560]{1,0:T(8,128)(2,1)S(1)} %collective-permute-done.1.refs_2_, bf16[16,2560]{1,0:T(8,128)(2,1)S(1)} %collective-permute-done.2.refs_3_, ...), custom_call_target="tpu_custom_call" | custom-call | tf_op jit(solution)/shard_map/pallas_call | solution.py:457
Async XLA Ops:
  17.2 12.8 %collective-permute-start = (bf16[16,2560]{1,0:T(8,128)(2,1)S(1)}, bf16[16,2560]{1,0:T(8,128)(2,1)S(1)}, u32[]{:S(2)}, u32[]{:S(2)}) collective-permute-start(bf16[16,2560]{1,0:T(8,128)(2,1)S(1)} %get-tuple-element.13), channel_id=1, source_target_pairs={{0,4},{4,0},{8,12},{12,8},{1,5},{5,1},{9,13},{13,9},{2,6},{6,2},{1... | collective-permute-start | bytes 245768 | tf_op jit(solution)/shard_map/ppermute | solution.py:443
  19.6 10.4 %collective-permute-start.1 = (bf16[16,2560]{1,0:T(8,128)(2,1)S(1)}, bf16[16,2560]{1,0:T(8,128)(2,1)S(1)}, u32[]{:S(2)}, u32[]{:S(2)}) collective-permute-start(bf16[16,2560]{1,0:T(8,128)(2,1)S(1)} %get-tuple-element.14), channel_id=1, source_target_pairs={{0,8},{4,12},{8,0},{12,4},{1,9},{5,13},{9,1},{13,5},{2,10},{6,14},... | collective-permute-start | bytes 245768 | tf_op jit(solution)/shard_map/ppermute | solution.py:443
  22.3 7.8 %collective-permute-start.2 = (bf16[16,2560]{1,0:T(8,128)(2,1)S(1)}, bf16[16,2560]{1,0:T(8,128)(2,1)S(1)}, u32[]{:S(2)}, u32[]{:S(2)}) collective-permute-start(bf16[16,2560]{1,0:T(8,128)(2,1)S(1)} %get-tuple-element.15), channel_id=1, source_target_pairs={{0,12},{4,8},{8,4},{12,0},{1,13},{5,9},{9,5},{13,1},{2,14},{6,10},... | collective-permute-start | bytes 245768 | tf_op jit(solution)/shard_map/ppermute | solution.py:443
  22.3 7.8 %copy-start = (f32[16,2304]{1,0:T(8,128)S(1)}, f32[16,2304]{1,0:T(8,128)}, u32[]{:S(2)}) copy-start(f32[16,2304]{1,0:T(8,128)} %refs_5_.1) | copy-start | bytes 442372
  22.3 7.8 %copy-start.1 = (s32[16,18]{1,0:T(8,128)S(1)}, s32[16,18]{1,0:T(8,128)}, u32[]{:S(2)}) copy-start(s32[16,18]{1,0:T(8,128)} %refs_6_.1) | copy-start | bytes 3460

commit v4 on v3

--- a/solution.py
+++ b/solution.py
@@ -250,9 +250,9 @@
             rowd[...].reshape(n * depth, tile), old[:, at].astype(jnp.bfloat16), preferred_element_type=jnp.float32
         )
         pack[:, :, at] = value.astype(jnp.bfloat16).reshape(n, depth, span)
-        if p < n - 1:
-            tokens_step(p)
-    for i in range(parts, n - 1):
+        if p % 2 == 1 and p // 2 < n - 1:
+            tokens_step(p // 2)
+    for i in range(parts // 2, n - 1):
         tokens_step(i)
 
     @pl.when(twin)
@@ -400,7 +400,7 @@
     vmem = pl.BlockSpec(memory_space=pltpu.VMEM)
     dma = pltpu.SemaphoreType.DMA
     hbm = pl.BlockSpec(memory_space=pltpu.HBM)
-    parts = 3 if tile % 384 == 0 else 1
+    parts = 6 if tile % 768 == 0 else 1
     wide = tile + 2 * n * held + 128
     old, colp, rowt, *packs = pl.pallas_call(
         functools.partial(gather_kernel, n, parts),
@@ -442,13 +442,13 @@
     got = [packs[0]] + [
         lax.ppermute(packs[k], "row", [(i, swap(i, k)) for i in range(n)]) for k in range(1, n)
     ]
-    rows = 256 if tile % 256 == 0 else 128
+    rows = 128
     hessian = pl.pallas_call(
         functools.partial(main_kernel, rows),
         out_shape=jax.ShapeDtypeStruct((tile, tile), jnp.float32),
         in_specs=[vmem] * 3,
         out_specs=hbm,
-        scratch_shapes=[pltpu.VMEM((3, rows, tile), jnp.float32), dma((3,))],
+        scratch_shapes=[pltpu.VMEM((6, rows, tile), jnp.float32), dma((6,))],
         compiler_params=pltpu.CompilerParams(vmem_limit_bytes=12 << 20),
         cost_estimate=pl.CostEstimate(
             flops=2 * n * held * tile * tile, bytes_accessed=8 * tile * tile, transcendentals=0

time: 31.4 us -> 30.8 us (0.981)
  no operation moved by 1% of the time
where the time goes in v4:
time: 30.8 us; the launch traced here: 30.7 us
  Pallas kernels  25.1 us (81%)
  starting transfers between devices  4.93 us (16%)
  between operations  0.69 us (2%)
    pallas_call x1, Pallas kernels, fused(): pl.pallas_call(functools.partial(gather_kernel, n, parts), out_shape=(jax...  16.5 us
    pallas_call x1, Pallas kernels, fused(): pl.pallas_call(functools.partial(main_kernel, rows), out_shape=jax.ShapeD...  7.58 us
    ppermute x3, starting transfers between devices, fused(): lax.ppermute(packs[k], 'row', [(i, swap(i, k)) for i in range(n)])  4.93 us
    pallas_call x1, Pallas kernels, fused(): pl.pallas_call(functools.partial(step_kernel, n), out_shape=jax.ShapeDtyp...  0.96 us
  transfers between devices with their start and end apart: 3, of which 0 were waited for; matrix products, arithmetic and copies ran while one was open for 0% of the time, Pallas kernels for 25%

profile of v4, /device:TPU:0, one launch (start us, length us, event | category | flops | bytes accessed | tf_op | source)
XLA Modules:
  0.0 30.7 jit_solution(14697438826757753299)
XLA Ops:
  0.6 16.5 %shard_map.68 = (f32[2304,2304]{1,0:T(8,128)S(1)}, bf16[4,16,2304]{2,1,0:T(8,128)(2,1)S(1)}, bf16[4,16,2304]{2,1,0:T(8,128)(2,1)S(1)}, bf16[16,2560]{1,0:T(8,128...) custom-call(f32[2304,2304]{1,0:T(8,128)} %old_hbm.1, ...), custom_call_target="tpu_custom_call" | custom-call | tf_op jit(solution)/shard_map/pallas_call | solution.py:405
  17.2 2.5 %collective-permute-start = (bf16[16,2560]{1,0:T(8,128)(2,1)S(1)}, bf16[16,2560]{1,0:T(8,128)(2,1)S(1)}, u32[]{:S(2)}, u32[]{:S(2)}) collective-permute-start(bf16[16,2560]{1,0:T(8,128)(2,1)S(1)} %get-tuple-element.13), channel_id=1, source_target_pairs={{0,4},{4,0},{8,12},{12,8},{1,5},{5,1},{9,13},{13,9},{2,6},{6,2},{1... | collective-permute-start | bytes 245768 | tf_op jit(solution)/shard_map/ppermute | solution.py:443
  19.6 2.5 %collective-permute-start.1 = (bf16[16,2560]{1,0:T(8,128)(2,1)S(1)}, bf16[16,2560]{1,0:T(8,128)(2,1)S(1)}, u32[]{:S(2)}, u32[]{:S(2)}) collective-permute-start(bf16[16,2560]{1,0:T(8,128)(2,1)S(1)} %get-tuple-element.14), channel_id=1, source_target_pairs={{0,8},{4,12},{8,0},{12,4},{1,9},{5,13},{9,1},{13,5},{2,10},{6,14},... | collective-permute-start | bytes 245768 | tf_op jit(solution)/shard_map/ppermute | solution.py:443
  22.1 0.0 collective-permute-start.2
  22.1 0.0 copy-start
  22.1 0.0 copy-start.1
  22.1 7.6 %shard_map.69 = f32[2304,2304]{1,0:T(8,128)} custom-call(f32[2304,2304]{1,0:T(8,128)S(1)} %get-tuple-element.9.old_ref, bf16[64,2304]{1,0:T(8,128)(2,1)S(1)} %bitcast.4, bf16[64,2304]{1,0:T(8,128)(2,1)S(1)} %bitcast.2), custom_call_target="tpu_custom_call" | custom-call | flops 679477248 | bytes 42467328 | tf_op jit(solution)/shard_map/pallas_call | solution.py:446
  29.7 0.0 collective-permute-done.refs_1_
  29.7 0.0 collective-permute-done.1.refs_2_
  29.7 0.0 collective-permute-done.2.refs_3_
  29.7 0.0 copy-done
  29.7 0.0 copy-done.1
  29.7 1.0 %shard_map.70 = f32[16,2304]{1,0:T(8,128)} custom-call(bf16[16,2560]{1,0:T(8,128)(2,1)S(1)} %get-tuple-element.12.refs_0_, bf16[16,2560]{1,0:T(8,128)(2,1)S(1)} %collective-permute-done.refs_1_, bf16[16,2560]{1,0:T(8,128)(2,1)S(1)} %collective-permute-done.1.refs_2_, bf16[16,2560]{1,0:T(8,128)(2,1)S(1)} %collective-permute-done.2.refs_3_, ...), custom_call_target="tpu_custom_call" | custom-call | tf_op jit(solution)/shard_map/pallas_call | solution.py:457
Async XLA Ops:
  17.2 12.5 %collective-permute-start = (bf16[16,2560]{1,0:T(8,128)(2,1)S(1)}, bf16[16,2560]{1,0:T(8,128)(2,1)S(1)}, u32[]{:S(2)}, u32[]{:S(2)}) collective-permute-start(bf16[16,2560]{1,0:T(8,128)(2,1)S(1)} %get-tuple-element.13), channel_id=1, source_target_pairs={{0,4},{4,0},{8,12},{12,8},{1,5},{5,1},{9,13},{13,9},{2,6},{6,2},{1... | collective-permute-start | bytes 245768 | tf_op jit(solution)/shard_map/ppermute | solution.py:443
  19.6 10.1 %collective-permute-start.1 = (bf16[16,2560]{1,0:T(8,128)(2,1)S(1)}, bf16[16,2560]{1,0:T(8,128)(2,1)S(1)}, u32[]{:S(2)}, u32[]{:S(2)}) collective-permute-start(bf16[16,2560]{1,0:T(8,128)(2,1)S(1)} %get-tuple-element.14), channel_id=1, source_target_pairs={{0,8},{4,12},{8,0},{12,4},{1,9},{5,13},{9,1},{13,5},{2,10},{6,14},... | collective-permute-start | bytes 245768 | tf_op jit(solution)/shard_map/ppermute | solution.py:443
  22.1 7.6 %collective-permute-start.2 = (bf16[16,2560]{1,0:T(8,128)(2,1)S(1)}, bf16[16,2560]{1,0:T(8,128)(2,1)S(1)}, u32[]{:S(2)}, u32[]{:S(2)}) collective-permute-start(bf16[16,2560]{1,0:T(8,128)(2,1)S(1)} %get-tuple-element.15), channel_id=1, source_target_pairs={{0,12},{4,8},{8,4},{12,0},{1,13},{5,9},{9,5},{13,1},{2,14},{6,10},... | collective-permute-start | bytes 245768 | tf_op jit(solution)/shard_map/ppermute | solution.py:443
  22.1 7.6 %copy-start = (f32[16,2304]{1,0:T(8,128)S(1)}, f32[16,2304]{1,0:T(8,128)}, u32[]{:S(2)}) copy-start(f32[16,2304]{1,0:T(8,128)} %refs_5_.1) | copy-start | bytes 442372
  22.1 7.6 %copy-start.1 = (s32[16,18]{1,0:T(8,128)S(1)}, s32[16,18]{1,0:T(8,128)}, u32[]{:S(2)}) copy-start(s32[16,18]{1,0:T(8,128)} %refs_6_.1) | copy-start | bytes 3460

commit v5 on v4

--- a/solution.py
+++ b/solution.py
@@ -163,7 +163,7 @@
     def got_diff(s):
         remote(diff, rowd.at[s], send_d, recv_d.at[s], partner_dev).wait_recv()
 
-    late = lax.rem(c, 2) == 1
+    late = jnp.logical_and(lax.rem(c, 2) == 1, crosses)
 
     def tokens_out(first):
         if first:
@@ -380,6 +380,8 @@
     both = jnp.concatenate([high, low.astype(jnp.bfloat16)], axis=0)
     blocks = m_ref.shape[1]
     width = tile // blocks
+    stops = [0, blocks] if blocks == 1 else [0, (blocks + 1) // 2, blocks]
+    copies = []
     for b in range(blocks):
         at = slice(b * width, (b + 1) * width)
         value = jnp.dot(both, cp_ref[:, at], preferred_element_type=jnp.float32)
@@ -388,9 +390,13 @@
             grad = grad + got[s][:, at].astype(jnp.float32)
         kept = m_ref[:, b : b + 1].astype(jnp.float32)
         new[:, at] = kept * (w_ref[:, at] - step * grad)
-    last = pltpu.make_async_copy(new, new_hbm, new_sem)
-    last.start()
-    last.wait()
+        if b + 1 in stops:
+            done = slice(stops[stops.index(b + 1) - 1] * width, (b + 1) * width)
+            copy = pltpu.make_async_copy(new.at[:, done], new_hbm.at[:, done], new_sem.at[len(copies)])
+            copy.start()
+            copies.append(copy)
+    for copy in copies:
+        copy.wait()
 
 
 def fused(n, hessian_old, tokens, weight, dense_weight, block_mask):
@@ -459,7 +465,7 @@
         out_shape=jax.ShapeDtypeStruct((depth, tile), jnp.float32),
         in_specs=[vmem] * (n + 3),
         out_specs=hbm,
-        scratch_shapes=[pltpu.VMEM((depth, tile), jnp.float32), dma],
+        scratch_shapes=[pltpu.VMEM((depth, tile), jnp.float32), dma((2,))],
         compiler_params=pltpu.CompilerParams(vmem_limit_bytes=4 << 20),
     )(*got, colp, weight, block_mask)
     return hessian, new_weight

time: 30.8 us -> 30.8 us (level)
  no operation moved by 1% of the time
where the time goes in v5:
time: 30.8 us; the launch traced here: 30.7 us
  Pallas kernels  25 us (81%)
  starting transfers between devices  4.93 us (16%)
  between operations  0.69 us (2%)
    pallas_call x1, Pallas kernels, fused(): pl.pallas_call(functools.partial(gather_kernel, n, parts), out_shape=(jax...  16.5 us
    pallas_call x1, Pallas kernels, fused(): pl.pallas_call(functools.partial(main_kernel, rows), out_shape=jax.ShapeD...  7.58 us
    ppermute x3, starting transfers between devices, fused(): lax.ppermute(packs[k], 'row', [(i, swap(i, k)) for i in range(n)])  4.93 us
    pallas_call x1, Pallas kernels, fused(): pl.pallas_call(functools.partial(step_kernel, n), out_shape=jax.ShapeDtyp...  0.94 us
  transfers between devices with their start and end apart: 3, of which 0 were waited for; matrix products, arithmetic and copies ran while one was open for 0% of the time, Pallas kernels for 25%

profile of v5, /device:TPU:0, one launch (start us, length us, event | category | flops | bytes accessed | tf_op | source)
XLA Modules:
  0.0 30.7 jit_solution(566780647610318)
XLA Ops:
  0.6 16.5 %shard_map.68 = (f32[2304,2304]{1,0:T(8,128)S(1)}, bf16[4,16,2304]{2,1,0:T(8,128)(2,1)S(1)}, bf16[4,16,2304]{2,1,0:T(8,128)(2,1)S(1)}, bf16[16,2560]{1,0:T(8,128...) custom-call(f32[2304,2304]{1,0:T(8,128)} %old_hbm.1, ...), custom_call_target="tpu_custom_call" | custom-call | tf_op jit(solution)/shard_map/pallas_call | solution.py:411
  17.2 2.5 %collective-permute-start = (bf16[16,2560]{1,0:T(8,128)(2,1)S(1)}, bf16[16,2560]{1,0:T(8,128)(2,1)S(1)}, u32[]{:S(2)}, u32[]{:S(2)}) collective-permute-start(bf16[16,2560]{1,0:T(8,128)(2,1)S(1)} %get-tuple-element.13), channel_id=1, source_target_pairs={{0,4},{4,0},{8,12},{12,8},{1,5},{5,1},{9,13},{13,9},{2,6},{6,2},{1... | collective-permute-start | bytes 245768 | tf_op jit(solution)/shard_map/ppermute | solution.py:449
  19.6 2.5 %collective-permute-start.1 = (bf16[16,2560]{1,0:T(8,128)(2,1)S(1)}, bf16[16,2560]{1,0:T(8,128)(2,1)S(1)}, u32[]{:S(2)}, u32[]{:S(2)}) collective-permute-start(bf16[16,2560]{1,0:T(8,128)(2,1)S(1)} %get-tuple-element.14), channel_id=1, source_target_pairs={{0,8},{4,12},{8,0},{12,4},{1,9},{5,13},{9,1},{13,5},{2,10},{6,14},... | collective-permute-start | bytes 245768 | tf_op jit(solution)/shard_map/ppermute | solution.py:449
  22.1 0.0 collective-permute-start.2
  22.1 0.0 copy-start
  22.1 0.0 copy-start.1
  22.1 7.6 %shard_map.69 = f32[2304,2304]{1,0:T(8,128)} custom-call(f32[2304,2304]{1,0:T(8,128)S(1)} %get-tuple-element.9.old_ref, bf16[64,2304]{1,0:T(8,128)(2,1)S(1)} %bitcast.4, bf16[64,2304]{1,0:T(8,128)(2,1)S(1)} %bitcast.2), custom_call_target="tpu_custom_call" | custom-call | flops 679477248 | bytes 42467328 | tf_op jit(solution)/shard_map/pallas_call | solution.py:452
  29.7 0.0 collective-permute-done.refs_1_
  29.7 0.0 collective-permute-done.1.refs_2_
  29.7 0.0 collective-permute-done.2.refs_3_
  29.7 0.0 copy-done
  29.7 0.0 copy-done.1
  29.7 0.9 %shard_map.70 = f32[16,2304]{1,0:T(8,128)} custom-call(bf16[16,2560]{1,0:T(8,128)(2,1)S(1)} %get-tuple-element.12.refs_0_, bf16[16,2560]{1,0:T(8,128)(2,1)S(1)} %collective-permute-done.refs_1_, bf16[16,2560]{1,0:T(8,128)(2,1)S(1)} %collective-permute-done.1.refs_2_, bf16[16,2560]{1,0:T(8,128)(2,1)S(1)} %collective-permute-done.2.refs_3_, ...), custom_call_target="tpu_custom_call" | custom-call | tf_op jit(solution)/shard_map/pallas_call | solution.py:463
Async XLA Ops:
  17.2 12.5 %collective-permute-start = (bf16[16,2560]{1,0:T(8,128)(2,1)S(1)}, bf16[16,2560]{1,0:T(8,128)(2,1)S(1)}, u32[]{:S(2)}, u32[]{:S(2)}) collective-permute-start(bf16[16,2560]{1,0:T(8,128)(2,1)S(1)} %get-tuple-element.13), channel_id=1, source_target_pairs={{0,4},{4,0},{8,12},{12,8},{1,5},{5,1},{9,13},{13,9},{2,6},{6,2},{1... | collective-permute-start | bytes 245768 | tf_op jit(solution)/shard_map/ppermute | solution.py:449
  19.6 10.1 %collective-permute-start.1 = (bf16[16,2560]{1,0:T(8,128)(2,1)S(1)}, bf16[16,2560]{1,0:T(8,128)(2,1)S(1)}, u32[]{:S(2)}, u32[]{:S(2)}) collective-permute-start(bf16[16,2560]{1,0:T(8,128)(2,1)S(1)} %get-tuple-element.14), channel_id=1, source_target_pairs={{0,8},{4,12},{8,0},{12,4},{1,9},{5,13},{9,1},{13,5},{2,10},{6,14},... | collective-permute-start | bytes 245768 | tf_op jit(solution)/shard_map/ppermute | solution.py:449
  22.1 7.6 %collective-permute-start.2 = (bf16[16,2560]{1,0:T(8,128)(2,1)S(1)}, bf16[16,2560]{1,0:T(8,128)(2,1)S(1)}, u32[]{:S(2)}, u32[]{:S(2)}) collective-permute-start(bf16[16,2560]{1,0:T(8,128)(2,1)S(1)} %get-tuple-element.15), channel_id=1, source_target_pairs={{0,12},{4,8},{8,4},{12,0},{1,13},{5,9},{9,5},{13,1},{2,14},{6,10},... | collective-permute-start | bytes 245768 | tf_op jit(solution)/shard_map/ppermute | solution.py:449
  22.1 7.6 %copy-start = (f32[16,2304]{1,0:T(8,128)S(1)}, f32[16,2304]{1,0:T(8,128)}, u32[]{:S(2)}) copy-start(f32[16,2304]{1,0:T(8,128)} %refs_5_.1) | copy-start | bytes 442372
  22.1 7.6 %copy-start.1 = (s32[16,18]{1,0:T(8,128)S(1)}, s32[16,18]{1,0:T(8,128)}, u32[]{:S(2)}) copy-start(s32[16,18]{1,0:T(8,128)} %refs_6_.1) | copy-start | bytes 3460
